TPU v7x, 32 devices: a whole 2x2x4 slice. The times are simulated.
32 devices in a mesh: seq: 8 (over z, y), head: 4 (over x, core).
Axes of the slice: x: 2, y: 2, z: 4, core: 2. Of those that a mesh axis runs over, the one named last changes fastest.
Arguments:
- queries: bfloat16 [4096, 4096], P('seq', 'head'), may hold values from -5 to 5
- keys: bfloat16 [4096, 1024], P('seq', 'head'), may hold values from -5 to 5
- values: bfloat16 [4096, 1024], P('seq', 'head'), may hold values from -5 to 5
- doc_lengths: int32 [16], replicated, may hold values from 1 to 2048, 4096 in all
- out_weight: bfloat16 [4096, 4096], P('head', 'seq'), may hold values from -0.125 to 0.125
Outputs:
- mixed: bfloat16 [4096, 4096], P('seq', 'head')
Inputs may be any that keep to these rules, and one draw needn't show every extreme that they name: `doc_lengths`: the lengths sum to 4096, and one document is exactly 2048 tokens long.
All inputs are finite; a program needn't handle non-finite values.
Results may differ from a plain program's by a relative error of at most 0.012.
Values may be sent and summed in bfloat16 or wider, within the bound.
A program may use at most 128 MiB of HBM per device.

v0:
```python
import math

import jax
import jax.numpy as jnp
from jax import lax
from jax.sharding import PartitionSpec as P

HQ = 32
KV = 8
DH = 128
REACH = 4


def from_behind(block, axis, distance):
    devices = range(lax.axis_size(axis))
    route = [(i - distance, i) for i in devices if i - distance in devices]
    return lax.ppermute(block, axis, route)


def doc_index(positions, starts):
    return jnp.sum((starts[None, :] <= positions[:, None]).astype(jnp.int32), axis=1) - 1


def body(queries, keys, values, doc_lengths, out_weight):
    local_rows = queries.shape[0]
    kv_local = keys.shape[1] // DH
    group_size = HQ // KV
    temper = DH ** (-0.5)
    starts = jnp.cumsum(doc_lengths) - doc_lengths
    q_first = lax.axis_index("seq") * local_rows
    q_pos = q_first + jnp.arange(local_rows, dtype=jnp.int32)
    q_doc = doc_index(q_pos, starts)
    q_heads = queries.reshape(local_rows, kv_local, group_size, DH)

    def attend(carry, piece, piece_start):
        key_piece, value_piece = piece
        key_count = key_piece.shape[0]
        block_len = math.gcd(key_count, 512)
        num_blocks = key_count // block_len
        key_blocks = key_piece.reshape(num_blocks, block_len, kv_local, DH)
        value_blocks = value_piece.reshape(num_blocks, block_len, kv_local, DH)
        block_starts = piece_start + block_len * jnp.arange(num_blocks, dtype=jnp.int32)

        def one_block(state, entry):
            key_block, value_block, block_first = entry
            k_pos = block_first + jnp.arange(block_len, dtype=jnp.int32)
            k_doc = doc_index(k_pos, starts)
            needed = (block_first >= 0) & (block_first <= q_pos[-1]) & (k_doc[-1] >= q_doc[0])

            def update(inner):
                row_max, row_sum, accum = inner
                scores = (
                    jnp.einsum(
                        "qkgd,nkd->kgqn", q_heads, key_block, preferred_element_type=jnp.float32
                    )
                    * temper
                )
                allowed = (k_doc[None, :] == q_doc[:, None]) & (k_pos[None, :] <= q_pos[:, None])
                scores = jnp.where(allowed[None, None], scores, jnp.float32(-1e30))
                new_max = jnp.maximum(row_max, jnp.max(scores, axis=-1))
                probs = jnp.where(
                    allowed[None, None], jnp.exp(scores - new_max[..., None]), jnp.float32(0.0)
                )
                fading = jnp.exp(row_max - new_max)
                row_sum = row_sum * fading + jnp.sum(probs, axis=-1)
                weights = probs.astype(jnp.bfloat16)
                accum = accum * fading[..., None] + jnp.einsum(
                    "kgqn,nkd->kgqd", weights, value_block, preferred_element_type=jnp.float32
                )
                return (new_max, row_sum, accum)

            def unchanged(inner):
                return inner

            return (lax.cond(needed, update, unchanged, state), None)

        carry, _ = lax.scan(one_block, carry, (key_blocks, value_blocks, block_starts))
        return carry

    initial = (
        jnp.full((kv_local, group_size, local_rows), -1e30, jnp.float32),
        jnp.zeros((kv_local, group_size, local_rows), jnp.float32),
        jnp.zeros((kv_local, group_size, local_rows, DH), jnp.float32),
    )
    final = attend(initial, (keys, values), q_first)
    paired = jnp.stack((keys, values))
    for offset in range(REACH):
        paired = from_behind(paired, "seq", 1)
        final = attend(final, (paired[0], paired[1]), q_first - (offset + 1) * local_rows)
    row_max, row_sum, accum = final
    attn = (accum / row_sum[..., None]).astype(jnp.bfloat16)
    attn = jnp.transpose(attn, (2, 0, 1, 3)).reshape(local_rows, kv_local * group_size * DH)
    partial_terms = jnp.dot(
        attn,
        lax.all_gather(out_weight, "seq", axis=1, tiled=True),
        preferred_element_type=jnp.float32,
    )
    return lax.psum_scatter(
        partial_terms.astype(jnp.bfloat16), "head", scatter_dimension=1, tiled=True
    )


def solution(mesh):
    return jax.shard_map(
        body,
        mesh=mesh,
        in_specs=(P("seq", "head"), P("seq", "head"), P("seq", "head"), P(), P("head", "seq")),
        out_specs=P("seq", "head"),
        check_vma=False,
    )
```

profile of v0, /device:TPU:24, one launch (start us, length us, event | category | flops | bytes accessed | tf_op | source)
XLA Modules:
  0.0 231.4 jit_solution(17083058643937626783)
XLA Ops:
  7.3 1.1 copy.53
  8.4 1.1 copy.55
  9.6 3.4 %collective-permute-start = (bf16[2,512,256]{1,2,0:T(8,128)(2,1)S(1)}, bf16[2,512,256]{1,2,0:T(8,128)(2,1)S(1)}, u32[]{:S(2)}, u32[]{:S(2)}) collective-permute-start(bf16[2,512,256]{1,2,0:T(8,128)(2,1)S(1)} %pad_maximum_fusion), channel_id=1, source_target_pairs={{0,4},{4,8},{8,12},{12,16},{16,20},{20,24},{24,28},{1,5},{5,9},{9,... | collective-permute-start | bytes 1572872 | tf_op jit(solution)/shard_map/ppermute | solution.py:17
  14.6 21.1 %collective-permute-done = bf16[2,512,256]{1,2,0:T(8,128)(2,1)S(1)} collective-permute-done((bf16[2,512,256]{1,2,0:T(8,128)(2,1)S(1)}, bf16[2,512,256]{1,2,0:T(8,128)(2,1)S(1)}, u32[]{:S(2)}, u32[]{:S(2)}) %collective-permute-start) | collective-permute-done | bytes 524320 | tf_op jit(solution)/shard_map/ppermute | solution.py:17
  35.7 1.9 collective-permute-start.1
  37.7 30.7 %collective-permute-done.1 = bf16[2,512,256]{1,2,0:T(8,128)(2,1)S(1)} collective-permute-done((bf16[2,512,256]{1,2,0:T(8,128)(2,1)S(1)}, bf16[2,512,256]{1,2,0:T(8,128)(2,1)S(1)}, u32[]{:S(2)}, u32[]{:S(2)}) %collective-permute-start.1) | collective-permute-done | bytes 524320 | tf_op jit(solution)/shard_map/ppermute | solution.py:17
  68.5 1.9 collective-permute-start.2
  70.4 11.9 %collective-permute-done.2 = bf16[2,512,256]{1,2,0:T(8,128)(2,1)} collective-permute-done((bf16[2,512,256]{1,2,0:T(8,128)(2,1)S(1)}, bf16[2,512,256]{1,2,0:T(8,128)(2,1)}, u32[]{:S(2)}, u32[]{:S(2)}) %collective-permute-start.2) | collective-permute-done | bytes 524320 | tf_op jit(solution)/shard_map/ppermute | solution.py:17
  82.3 1.9 collective-permute-start.3
  96.9 1.5 copy.54
  98.6 7.7 %conditional.5 = ((f32[2,4,512]{2,1,0:T(4,128)S(1)}, f32[2,4,512]{2,1,0:T(4,128)S(1)}, f32[2,4,512,128]{3,2,1,0:T(8,128)S(1)})) conditional(s32[]{:T(128)} %convert_element_type.72, (f32[2,4,512]{2,1,0:T(4,128)S(1)}, f32[2,4,512]{2,1,0:T(4,128)S(1)}, f32[2,4,512,128]{3,2,1,0:T(8,128)S(1)}) %tuple.52, (s32[512]{0:T(512)S(1)}, s32[512]{0:T(512)S(1)}, ...), branch_computations={%region_6.7_spmd, %region_7.10_spmd} | conditional | flops 1102848000 | bytes 33296444 | solution.py:75
  98.9 1.6 fusion
  100.5 2.0 fusion.2
  102.6 3.6 %multiply_add_fusion = f32[2,4,512,128]{3,2,1,0:T(8,128)S(1)} fusion(f32[2,4,512,128]{3,2,1,0:T(8,128)S(1)} %get-tuple-element.301, f32[2,512,512,4]{2,1,3,0:T(8,128)S(1)} %get-tuple-element.540, f32[2,4,512]{2,1,0:T(4,128)S(1)} %max.11, pred[512,512]{0,1:T(8,128)(4,1)S(1)} %compare_and_fusion, f32[2,4,512]{2,1,0:T(4,128)S(1)} %bitcast.225, ...), kind=kOutput, calls=%fused_computation.7 | convolution fusion | flops 548405248 | bytes 13139968 | tf_op jit(solution)/shard_map/while/body/eval_jaxpr/cond/branch_1_fun/kgqn,nkd->kgqd/dot_general | solution.py:67
  107.4 7.8 %conditional.6 = ((f32[2,4,512]{2,1,0:T(4,128)S(1)}, f32[2,4,512]{2,1,0:T(4,128)S(1)}, f32[2,4,512,128]{3,2,1,0:T(8,128)S(1)})) conditional(s32[]{:T(128)} %convert_element_type.71, (f32[2,4,512]{2,1,0:T(4,128)S(1)}, f32[2,4,512]{2,1,0:T(4,128)S(1)}, f32[2,4,512,128]{3,2,1,0:T(8,128)S(1)}) %get-tuple-element.599, (s32[512]{0:T(512)S(1)}, ...), branch_computations={%region_10.11_spmd, %region_11.14_spmd} | conditional | flops 1102848000 | bytes 32251936 | solution.py:75
  107.8 1.6 fusion.14
  109.5 2.0 fusion.16
  111.5 3.6 %multiply_add_fusion.2 = f32[2,4,512,128]{3,2,1,0:T(8,128)S(1)} fusion(f32[2,4,512,128]{3,2,1,0:T(8,128)S(1)} %get-tuple-element.332, f32[2,512,512,4]{2,1,3,0:T(8,128)S(1)} %get-tuple-element.542, f32[2,4,512]{2,1,0:T(4,128)S(1)} %max.12, pred[512,512]{0,1:T(8,128)(4,1)S(1)} %compare_and_fusion.1, f32[2,4,512]{2,1,0:T(4,128)S(1)} %bitcast.226, ...), kind=kOutput, calls=%fused_computation.24 | convolution fusion | flops 548405248 | bytes 13139968 | tf_op jit(solution)/shard_map/while/body/eval_jaxpr/cond/branch_1_fun/kgqn,nkd->kgqd/dot_general | solution.py:67
  116.6 1.8 conditional.9
  116.6 1.8 copy.110
  118.4 1.9 divide_convert_fusion
  120.3 46.9 %all-gather.2.cloned.1.call-done = bf16[1024,4096]{1,0:T(8,128)(2,1)} async-done(((bf16[1024,512]{1,0:T(8,128)(2,1)}), bf16[1024,4096]{1,0:T(8,128)(2,1)}) %all-gather.2.cloned.1.call-update) | async-done | bytes 8388624 | tf_op jit(solution)/shard_map/all_gather | solution.py:95
  167.2 9.5 %convolution_convert_fusion = bf16[512,4096]{1,0:T(8,128)(2,1)} fusion(bf16[512,1024]{0,1:T(8,128)(2,1)S(1)} %bitcast.193, bf16[1024,4096]{1,0:T(8,128)(2,1)} %all-gather.2.cloned.1.call-done), kind=kOutput, calls=%fused_computation.81 | convolution fusion | flops 4297064448 | bytes 13631488 | tf_op jit(solution)/shard_map/dot_general | solution.py:93
  176.7 47.9 %reduce-scatter.2.cloned.1.call-done = bf16[512,1024]{1,0:T(8,128)(2,1)} async-done(((bf16[512,4096]{1,0:T(8,128)(2,1)}), bf16[512,1024]{1,0:T(8,128)(2,1)}) %reduce-scatter.2.cloned.1.call-update) | async-done | bytes 1048592 | tf_op jit(solution)/shard_map/reduce_scatter | solution.py:98
  (51 shorter events, 9.3 us)
Async XLA Ops:
  6.5 160.6 %all-gather.2.cloned.1.call-start = ((), (), s32[]{:S(2)}) async-start(), calls=%async_computation.1 | async-start | bytes 9437184 | tf_op jit(solution)/shard_map/all_gather | solution.py:95
  7.3 217.3 %reduce-scatter.2.cloned.1.call-start = ((), (), s32[]{:S(2)}) async-start(), calls=%async_computation.2 | async-start | bytes 5242880 | tf_op jit(solution)/shard_map/reduce_scatter | solution.py:98
  9.5 88.9 %copy-start = (bf16[512,256]{0,1:T(8,128)(2,1)}, bf16[512,256]{0,1:T(8,128)(2,1)S(1)}, u32[]{:S(2)}) copy-start(bf16[512,256]{0,1:T(8,128)(2,1)S(1)} %copy.55) | copy-start | bytes 786436
  9.6 26.1 %collective-permute-start = (bf16[2,512,256]{1,2,0:T(8,128)(2,1)S(1)}, bf16[2,512,256]{1,2,0:T(8,128)(2,1)S(1)}, u32[]{:S(2)}, u32[]{:S(2)}) collective-permute-start(bf16[2,512,256]{1,2,0:T(8,128)(2,1)S(1)} %pad_maximum_fusion), channel_id=1, source_target_pairs={{0,4},{4,8},{8,12},{12,16},{16,20},{20,24},{24,28},{1,5},{5,9},{9,... | collective-permute-start | bytes 1572872 | tf_op jit(solution)/shard_map/ppermute | solution.py:17
  35.7 62.7 %copy-start.3 = (bf16[2,512,256]{1,2,0:T(8,128)(2,1)}, bf16[2,512,256]{1,2,0:T(8,128)(2,1)S(1)}, u32[]{:S(2)}) copy-start(bf16[2,512,256]{1,2,0:T(8,128)(2,1)S(1)} %collective-permute-done) | copy-start | bytes 1572868
  35.7 32.8 %collective-permute-start.1 = (bf16[2,512,256]{1,2,0:T(8,128)(2,1)S(1)}, bf16[2,512,256]{1,2,0:T(8,128)(2,1)S(1)}, u32[]{:S(2)}, u32[]{:S(2)}) collective-permute-start(bf16[2,512,256]{1,2,0:T(8,128)(2,1)S(1)} %collective-permute-done), channel_id=1, source_target_pairs={{0,4},{4,8},{8,12},{12,16},{16,20},{20,24},{24,28},{1,5},{5,9},{9,... | collective-permute-start | bytes 1572872 | tf_op jit(solution)/shard_map/ppermute | solution.py:17
  68.5 29.9 %copy-start.2 = (bf16[2,512,256]{1,2,0:T(8,128)(2,1)}, bf16[2,512,256]{1,2,0:T(8,128)(2,1)S(1)}, u32[]{:S(2)}) copy-start(bf16[2,512,256]{1,2,0:T(8,128)(2,1)S(1)} %collective-permute-done.1) | copy-start | bytes 1572868
  68.5 13.8 %collective-permute-start.2 = (bf16[2,512,256]{1,2,0:T(8,128)(2,1)S(1)}, bf16[2,512,256]{1,2,0:T(8,128)(2,1)}, u32[]{:S(2)}, u32[]{:S(2)}) collective-permute-start(bf16[2,512,256]{1,2,0:T(8,128)(2,1)S(1)} %collective-permute-done.1), channel_id=1, source_target_pairs={{0,4},{4,8},{8,12},{12,16},{16,20},{20,24},{24,28},{1,5},{5,9},{9,... | collective-permute-start | bytes 1572872 | tf_op jit(solution)/shard_map/ppermute | solution.py:17
  82.3 34.2 %collective-permute-start.3 = (bf16[2,512,256]{1,2,0:T(8,128)(2,1)}, bf16[2,512,256]{1,2,0:T(8,128)(2,1)}, u32[]{:S(2)}, u32[]{:S(2)}) collective-permute-start(bf16[2,512,256]{1,2,0:T(8,128)(2,1)} %collective-permute-done.2), channel_id=1, source_target_pairs={{0,4},{4,8},{8,12},{12,16},{16,20},{20,24},{24,28},{1,5},{5,9},{9,... | collective-permute-start | bytes 1572872 | tf_op jit(solution)/shard_map/ppermute | solution.py:17
  98.9 3.7 %copy-start.1 = (bf16[512,2,128]{0,2,1:T(8,128)(2,1)S(1)}, bf16[512,2,128]{0,2,1:T(8,128)(2,1)}, u32[]{:S(2)}) copy-start(bf16[512,2,128]{0,2,1:T(8,128)(2,1)} %get-tuple-element.480) | copy-start | bytes 786436 | tf_op jit(solution)/shard_map/while/body/eval_jaxpr/cond
Sparse Core Ops, SparseCore 0:
  9.4 157.7 all-gather.1
  176.8 47.7 reduce-scatter.1
where the time goes:
time: 234 us; the launch traced here: 231 us
  waiting for transfers between devices  159 us (68%)
  between operations  22.6 us (10%)
  matrix products  20 us (9%)
  local copies, waits for them, and re-layouts  12.2 us (5%)
  starting transfers between devices  9.2 us (4%)
  other arithmetic  7.57 us (3%)
    ppermute x4, waiting for transfers between devices, from_behind(): return lax.ppermute(block, axis, route)  63.7 us
    reduce_scatter x1, waiting for transfers between devices, body(): lax.psum_scatter(partial_terms.astype(jnp.bfloat16), 'head', scatter_dime...  47.9 us
    all_gather x1, waiting for transfers between devices, body(): lax.all_gather(out_weight, 'seq', axis=1, tiled=True)  46.9 us
    dot_general x1, matrix products, body(): jnp.dot(attn, lax.all_gather(out_weight, 'seq', axis=1, tiled=True), pref...  9.46 us
    ppermute x4, starting transfers between devices, from_behind(): return lax.ppermute(block, axis, route)  9.16 us
    dot_general x2, matrix products, update(): jnp.einsum('kgqn,nkd->kgqd', weights, value_block, preferred_element_type...  7.3 us
  transfers between devices with their start and end apart: 6, of which 5 were waited for; matrix products, arithmetic and copies ran while one was open for 13% of the time, Pallas kernels for 0%

commit v1 on v0

v1 whole, which is shorter than its diff:
```python
import functools
import math

import jax
import jax.numpy as jnp
from jax import lax
from jax.experimental import pallas as pl
from jax.experimental.pallas import tpu as pltpu
from jax.sharding import PartitionSpec as P

HQ = 32
KV = 8
DH = 128
MOST = 2048
CHUNKS = 4
MESH = pl.DeviceIdType.MESH


def kernel(
    n_seq, lens_ref, q_ref, k_hbm, v_hbm, w_hbm, out_ref,
    kbuf, vbuf, wbuf, bias, vt, mx, sm, acc, attn, peer,
    give1, got1, keep, give2, got2, give3, got3,
    load_sem, kvz_send, kvy_send, kv_recv, wl_send, wl_recv, wr_send, wr_recv,
    at_send, at_recv, s1_send, s1_recv, s2_send, s2_recv, s3_send, s3_recv,
):
    s, h = lax.axis_index("seq"), lax.axis_index("head")
    pairs = n_seq // 2
    p, m = s // 2, lax.rem(s, 2)
    mate = s + 1 - 2 * m
    right = lax.rem(p + 1, pairs) * 2 + m
    left = lax.rem(p + pairs - 1, pairs) * 2 + m
    near = h + 1 - 2 * lax.rem(h, 2)
    far = lax.rem(h + 2, 4)
    rows = q_ref.shape[0]
    depth, wc = w_hbm.shape
    half = depth // 2
    groups = pairs // 4
    group_size = HQ // KV
    n_left = pairs // 2
    n_right = pairs - 1 - n_left
    part = rows * 2 // CHUNKS
    scale = DH ** (-0.5) * math.log2(math.e)

    def copy(src, dst, send, recv, seq, head):
        return pltpu.make_async_remote_copy(
            src_ref=src, dst_ref=dst, send_sem=send, recv_sem=recv,
            device_id={"seq": seq, "head": head}, device_id_type=MESH,
        )

    def kv_copies(src_slot, dst_slot, j, send, target):
        cols = pl.ds(pl.multiple_of(j * DH, DH), DH)
        return [
            copy(buf.at[src_slot, :, cols], buf.at[dst_slot, :, cols],
                 send.at[j, c], kv_recv.at[dst_slot, j, c], target, h)
            for c, buf in enumerate((kbuf, vbuf))
        ]

    def w_copy(block, part_at, step, send, recv, target):
        piece = wbuf.at[block, pl.ds(part_at * half, half)]
        return copy(piece, piece, send.at[step, part_at], recv.at[step, part_at], target, h)

    def left_copy(step, part_at):
        return w_copy(lax.rem(p + step, pairs), part_at, step, wl_send, wl_recv, left)

    def right_copy(step, part_at):
        return w_copy(lax.rem(p - step + pairs, pairs), part_at, step, wr_send, wr_recv, right)

    loads = [
        pltpu.make_async_copy(k_hbm, kbuf.at[0], load_sem.at[0]),
        pltpu.make_async_copy(v_hbm, vbuf.at[0], load_sem.at[1]),
        pltpu.make_async_copy(w_hbm, wbuf.at[p], load_sem.at[2]),
    ]
    for load in loads:
        load.start()

    barrier = pltpu.get_barrier_semaphore()
    for seq, head in ((mate, h), (left, h), (right, h), (s, near), (s, far)):
        pl.semaphore_signal(barrier, inc=1, device_id={"seq": seq, "head": head}, device_id_type=MESH)
    pl.semaphore_wait(barrier, 5)

    loads[0].wait()
    loads[1].wait()
    has_next = s + 2 < n_seq
    for j in range(2):
        @pl.when(has_next)
        def _():
            for c in kv_copies(0, 2, j, kvz_send.at[0], right):
                c.start()

        @pl.when(m == 0)
        def _():
            for c in kv_copies(0, 1, j, kvy_send.at[0], mate):
                c.start()

    loads[2].wait()
    for a in range(2):
        left_copy(0, a).start()

    q_pos = s * rows + lax.broadcasted_iota(jnp.int32, (1, rows), 1)
    start = jnp.int32(0)
    first = jnp.zeros((1, rows), jnp.int32)
    for d in range(1, lens_ref.shape[0]):
        start = start + lens_ref[d - 1]
        first = jnp.where(q_pos >= start, start, first)

    def finish(j):
        def one(g, _):
            i = j * group_size + g
            full = jnp.transpose(acc[i] / sm[i])
            attn[j, :, pl.ds(pl.multiple_of(g * DH, DH), DH)] = full.astype(jnp.bfloat16)
            return 0

        lax.fori_loop(0, group_size, one, 0)
        copy(attn.at[j], peer.at[j], at_send.at[j], at_recv.at[j], mate, h).start()

    def step(i, _):
        k = jnp.maximum(i - 2, 0)
        w = lax.rem(k, 4)
        slot = jnp.where(i < 2, 0, 2 + 2 * (k // 4) - lax.rem(w, 2))
        j = jnp.where(i < 2, i, w // 2)

        @pl.when((i >= 2) & (s >= slot))
        def _():
            for c in kv_copies(slot, slot, j, kvz_send.at[0], right):
                c.wait_recv()

            @pl.when((slot == 2) & has_next)
            def _():
                for c in kv_copies(2, 4, j, kvz_send.at[1], right):
                    c.start()

            @pl.when(slot == 2)
            def _():
                for c in kv_copies(2, 3 - 2 * m, j, kvy_send.at[1], mate):
                    c.start()

            @pl.when((slot == 4) & (m == 1))
            def _():
                for c in kv_copies(4, 3, j, kvy_send.at[2], mate):
                    c.start()

        @pl.when(i == 4)
        def _():
            for a in range(2):
                right_copy(0, a).start()

        for at, a in ((5, 0), (8, 1)):
            @pl.when(i == at)
            def _():
                left_copy(0, a).wait_recv()
                left_copy(1, a).start()

        @pl.when(s >= slot)
        def _():
            cols = pl.ds(pl.multiple_of(j * DH, DH), DH)
            k_pos = (s - slot) * rows + lax.broadcasted_iota(jnp.int32, (rows, rows), 0)
            bias[...] = jnp.where((k_pos >= first) & (k_pos <= q_pos), 0.0, -1e30)
            vt[...] = jnp.transpose(vbuf[slot, :, cols])

            def one(g, _):
                at = j * group_size + g
                q = q_ref[:, pl.ds(pl.multiple_of(at * DH, DH), DH)]
                scores = lax.dot_general(
                    kbuf[slot, :, cols], q, (((1,), (1,)), ((), ())),
                    preferred_element_type=jnp.float32,
                ) * scale + bias[...]
                top = jnp.max(scores, axis=0, keepdims=True)
                old = jnp.where(i < 2, jnp.full_like(top, -1e30), mx[at])
                new = jnp.maximum(old, top)
                probs = jnp.exp2(scores - new)
                fade = jnp.exp2(old - new)
                mx[at] = new
                total = jnp.sum(probs, axis=0, keepdims=True)
                sm[at] = jnp.where(i < 2, total, sm[at] * fade + total)
                mixed = jnp.dot(vt[...], probs.astype(jnp.bfloat16), preferred_element_type=jnp.float32)

                @pl.when(i < 2)
                def _():
                    acc[at] = mixed

                @pl.when(i >= 2)
                def _():
                    acc[at] = acc[at] * fade + mixed

                return 0

            lax.fori_loop(0, group_size, one, 0)

        for at, jj in ((7, 0), (9, 1)):
            @pl.when(i == at)
            def _():
                finish(jj)

        return 0

    lax.fori_loop(0, 10, step, 0)

    for t in range(1, max(n_left, n_right)):
        for a in range(2):
            if t < n_right:
                right_copy(t - 1, a).wait_recv()
                right_copy(t, a).start()
            if 2 <= t < n_left:
                left_copy(t - 1, a).wait_recv()
                left_copy(t, a).start()
    for a in range(2):
        right_copy(n_right - 1, a).wait_recv()
        left_copy(n_left - 1, a).wait_recv()

    def attn_copy(j):
        return copy(attn.at[j], peer.at[j], at_send.at[j], at_recv.at[j], mate, h)

    for j in range(2):
        attn_copy(j).wait_recv()

    def first_copy(r):
        return copy(give1.at[r], got1.at[r], s1_send.at[r], s1_recv.at[r], s, near)

    def second_copy(r):
        return copy(give2.at[r], got2.at[r], s2_send.at[r], s2_recv.at[r], s, far)

    def third_copy(r):
        return copy(give3.at[r], got3.at[r], s3_send.at[r], s3_recv.at[r], mate, h)

    per_side = CHUNKS // 2

    def product(source, at, group, store):
        x0 = source[0, pl.ds(at, part), :]
        x1 = source[1, pl.ds(at, part), :]
        for g in range(groups):
            block = group * groups + g
            store(g, jnp.dot(x0, wbuf[block, :half, :], preferred_element_type=jnp.float32)
                  + jnp.dot(x1, wbuf[block, half:, :], preferred_element_type=jnp.float32))

    def multiply(r, source, at):
        for x in range(2):
            def put(g, y, x=x):
                give1[r, x, :, g * wc:(g + 1) * wc] = y.astype(jnp.bfloat16)

            product(source, at, 2 * x + 1 - lax.rem(h, 2), put)
        first_copy(r).start()
        for x in range(2):
            def hold(g, y, x=x):
                keep[r, x, :, g * wc:(g + 1) * wc] = y

            product(source, at, 2 * x + lax.rem(h, 2), hold)

    mine, other = h // 2, 1 - h // 2

    def second(r):
        first_copy(r).wait_recv()
        give2[r] = (keep[r, other] + got1[r, other].astype(jnp.float32)).astype(jnp.bfloat16)
        second_copy(r).start()

    def result(r):
        second_copy(r).wait_recv()
        full = keep[r, mine] + got1[r, mine].astype(jnp.float32) + got2[r].astype(jnp.float32)
        return full.astype(jnp.bfloat16)

    def place(at, member, value):
        for mm in range(2):
            @pl.when(member == mm)
            def _():
                for g in range(groups):
                    c = (2 * g + mm) * wc
                    out_ref[pl.ds(at, part), c:c + wc] = value[:, g * wc:(g + 1) * wc]

    def round_trip(r, _):
        @pl.when(r < per_side)
        def _():
            multiply(r, peer, pl.multiple_of(r * part, part))

        @pl.when((r >= per_side) & (r < CHUNKS))
        def _():
            multiply(r, attn, pl.multiple_of((r - per_side) * part, part))

        @pl.when(r >= 1)
        def _():
            second(r - 1)

        return 0

    lax.fori_loop(0, CHUNKS + 1, round_trip, 0)

    for r in range(per_side):
        give3[r] = result(r)
        third_copy(r).start()
    for r in range(per_side, CHUNKS):
        place((r - per_side) * part, m, result(r))
    for r in range(per_side):
        third_copy(r).wait_recv()
        place(r * part, 1 - m, got3[r])

    for j in range(2):
        @pl.when(has_next)
        def _():
            for c in kv_copies(0, 2, j, kvz_send.at[0], right):
                c.wait_send()

        @pl.when((s >= 2) & has_next)
        def _():
            for c in kv_copies(2, 4, j, kvz_send.at[1], right):
                c.wait_send()

        @pl.when(m == 0)
        def _():
            for c in kv_copies(0, 1, j, kvy_send.at[0], mate):
                c.wait_send()

        @pl.when(s >= 2)
        def _():
            for c in kv_copies(2, 3 - 2 * m, j, kvy_send.at[1], mate):
                c.wait_send()

        @pl.when((s >= 4) & (m == 1))
        def _():
            for c in kv_copies(4, 3, j, kvy_send.at[2], mate):
                c.wait_send()

        attn_copy(j).wait_send()
        for t in range(n_left):
            left_copy(t, j).wait_send()
        for t in range(n_right):
            right_copy(t, j).wait_send()
    for r in range(CHUNKS):
        first_copy(r).wait_send()
        second_copy(r).wait_send()
    for r in range(per_side):
        third_copy(r).wait_send()


def body(n_seq, queries, keys, values, doc_lengths, out_weight):
    rows, width = queries.shape
    kv_width = keys.shape[1]
    depth, wc = out_weight.shape
    pairs = n_seq // 2
    n_left = pairs // 2
    n_right = pairs - 1 - n_left
    heads = width // DH
    part = rows * 2 // CHUNKS
    cw = pairs // 4 * wc
    slots = -(-(MOST - 1) // rows) + 1
    vmem = pl.BlockSpec(memory_space=pltpu.VMEM)
    hbm = pl.BlockSpec(memory_space=pl.ANY)
    bf, f32, dma = jnp.bfloat16, jnp.float32, pltpu.SemaphoreType.DMA
    return pl.pallas_call(
        functools.partial(kernel, n_seq),
        out_shape=jax.ShapeDtypeStruct((rows, wc * 2 * (pairs // 4)), bf),
        in_specs=[pl.BlockSpec(memory_space=pltpu.SMEM), vmem, hbm, hbm, hbm],
        out_specs=vmem,
        scratch_shapes=[
            pltpu.VMEM((slots, rows, kv_width), bf),
            pltpu.VMEM((slots, rows, kv_width), bf),
            pltpu.VMEM((pairs, depth, wc), bf),
            pltpu.VMEM((rows, rows), f32),
            pltpu.VMEM((DH, rows), bf),
            pltpu.VMEM((heads, 1, rows), f32),
            pltpu.VMEM((heads, 1, rows), f32),
            pltpu.VMEM((heads, DH, rows), f32),
            pltpu.VMEM((2, rows, width // 2), bf),
            pltpu.VMEM((2, rows, width // 2), bf),
            pltpu.VMEM((CHUNKS, 2, part, cw), bf),
            pltpu.VMEM((CHUNKS, 2, part, cw), bf),
            pltpu.VMEM((CHUNKS, 2, part, cw), f32),
            pltpu.VMEM((CHUNKS, part, cw), bf),
            pltpu.VMEM((CHUNKS, part, cw), bf),
            pltpu.VMEM((CHUNKS // 2, part, cw), bf),
            pltpu.VMEM((CHUNKS // 2, part, cw), bf),
            dma((3,)), dma((2, 2, 2)), dma((3, 2, 2)), dma((slots, 2, 2)),
            dma((n_left, 2)), dma((n_left, 2)), dma((n_right, 2)), dma((n_right, 2)),
            dma((2,)), dma((2,)), dma((CHUNKS,)), dma((CHUNKS,)),
            dma((CHUNKS,)), dma((CHUNKS,)), dma((CHUNKS // 2,)), dma((CHUNKS // 2,)),
        ],
        compiler_params=pltpu.CompilerParams(
            collective_id=0, has_side_effects=True, vmem_limit_bytes=56 * 1024 * 1024
        ),
    )(doc_lengths, queries, keys, values, out_weight)


def solution(mesh):
    return jax.shard_map(
        functools.partial(body, mesh.shape["seq"]),
        mesh=mesh,
        in_specs=(P("seq", "head"), P("seq", "head"), P("seq", "head"), P(), P("head", "seq")),
        out_specs=P("seq", "head"),
        check_vma=False,
    )
```

time: 234 us -> 125 us (0.53); the launches traced: 231 us -> 125 us
  waiting for transfers between devices: 159 us -> 0 us
  Pallas kernels: 0 us -> 123 us
  between operations: 22.6 us -> 0.01 us
  matrix products: 20 us -> 0 us
  local copies, waits for them, and re-layouts: 12.2 us -> 2.26 us
  starting transfers between devices: 9.2 us -> 0 us
  other arithmetic: 7.57 us -> 0 us
    pallas_call x0 -> x1, Pallas kernels: none -> 123 us  [body(): pl.pallas_call(functools.partial(kernel, n_seq), out_shape=jax.ShapeDtype...]
    ppermute x4 -> x0, waiting for transfers between devices: 63.7 us -> none  [from_behind(): return lax.ppermute(block, axis, route)]
    reduce_scatter x1 -> x0, waiting for transfers between devices: 47.9 us -> none  [body(): lax.psum_scatter(partial_terms.astype(jnp.bfloat16), 'head', scatter_dime...]
    all_gather x1 -> x0, waiting for transfers between devices: 46.9 us -> none  [body(): lax.all_gather(out_weight, 'seq', axis=1, tiled=True)]
    dot_general x5 -> x0, matrix products: 20 us -> none  [the longest x1 9.46 us: body(): jnp.dot(attn, lax.all_gather(out_weight, 'seq', axis=1, tiled=True), pref...]
    ppermute x4 -> x0, starting transfers between devices: 9.16 us -> none  [from_behind(): return lax.ppermute(block, axis, route)]
    slice x8 -> x0, local copies, waits for them, and re-layouts: 5.79 us -> none  [the longest x5 3.07 us: one_block(): k_doc[-1] >= q_doc[0]]
    reduce_sum x3 -> x0, other arithmetic: 4.21 us -> none  [the longest x2 4.09 us: update(): row_sum = row_sum * fading + jnp.sum(probs, axis=-1)]
  transfers between devices with their start and end apart: 6 -> 0, of which waited for: 5 -> 0; matrix products, arithmetic and copies ran while one was open for 13% -> 0% of each run, Pallas kernels for 0% -> 0%
where the time goes in v1:
time: 125 us
  Pallas kernels  123 us (98%)
  local copies, waits for them, and re-layouts  2.26 us (2%)
    pallas_call x1, Pallas kernels, body(): pl.pallas_call(functools.partial(kernel, n_seq), out_shape=jax.ShapeDtype...  123 us

profile of v1, /device:TPU:24, one launch (start us, length us, event | category | flops | bytes accessed | tf_op | source)
XLA Modules:
  0.0 125.3 jit_solution(10719025676962886309)
XLA Ops:
  0.0 123.0 %shard_map.55 = bf16[512,1024]{1,0:T(8,128)(2,1)} custom-call(s32[16]{0:T(128)} %lens_ref.1, bf16[512,1024]{1,0:T(8,128)(2,1)} %q_ref.1, bf16[512,256]{1,0:T(8,128)(2,1)} %k_hbm.1, bf16[512,256]{1,0:T(8,128)(2,1)} %v_hbm.1, bf16[1024,512]{1,0:T(8,128)(2,1)} %w_hbm.1), custom_call_target="tpu_custom_call" | custom-call | tf_op jit(solution)/shard_map/pallas_call | solution.py:346
  123.0 2.3 %copy.7 = bf16[512,1024]{1,0:T(8,128)(2,1)} copy(bf16[512,1024]{1,0:T(8,128)(2,1)} %shard_map.55) | data formatting | bytes 2097152

commit v2 on v1

--- a/solution.py
+++ b/solution.py
@@ -18,8 +18,8 @@
 
 def kernel(
     n_seq, lens_ref, q_ref, k_hbm, v_hbm, w_hbm, out_ref,
-    kbuf, vbuf, wbuf, bias, vt, mx, sm, acc, attn, peer,
-    give1, got1, keep, give2, got2, give3, got3,
+    kbuf, vbuf, wbuf, bias, vt, mx, sm, acc, both,
+    tmp, keep, sum1, sum2, give3, got3,
     load_sem, kvz_send, kvy_send, kv_recv, wl_send, wl_recv, wr_send, wr_recv,
     at_send, at_recv, s1_send, s1_recv, s2_send, s2_recv, s3_send, s3_recv,
 ):
@@ -36,9 +36,8 @@
     half = depth // 2
     groups = pairs // 4
     group_size = HQ // KV
-    n_left = pairs // 2
-    n_right = pairs - 1 - n_left
     part = rows * 2 // CHUNKS
+    has_up, has_down = p + 1 < pairs, p >= 1
     scale = DH ** (-0.5) * math.log2(math.e)
 
     def copy(src, dst, send, recv, seq, head):
@@ -60,10 +59,10 @@
         return copy(piece, piece, send.at[step, part_at], recv.at[step, part_at], target, h)
 
     def left_copy(step, part_at):
-        return w_copy(lax.rem(p + step, pairs), part_at, step, wl_send, wl_recv, left)
+        return w_copy(jnp.minimum(p + step, pairs - 1), part_at, step, wl_send, wl_recv, left)
 
     def right_copy(step, part_at):
-        return w_copy(lax.rem(p - step + pairs, pairs), part_at, step, wr_send, wr_recv, right)
+        return w_copy(jnp.maximum(p - step, 0), part_at, step, wr_send, wr_recv, right)
 
     loads = [
         pltpu.make_async_copy(k_hbm, kbuf.at[0], load_sem.at[0]),
@@ -93,8 +92,11 @@
                 c.start()
 
     loads[2].wait()
-    for a in range(2):
-        left_copy(0, a).start()
+
+    @pl.when(has_down)
+    def _():
+        for a in range(2):
+            left_copy(0, a).start()
 
     q_pos = s * rows + lax.broadcasted_iota(jnp.int32, (1, rows), 1)
     start = jnp.int32(0)
@@ -103,15 +105,18 @@
         start = start + lens_ref[d - 1]
         first = jnp.where(q_pos >= start, start, first)
 
+    def attn_copy(j):
+        return copy(both.at[1, j], both.at[0, j], at_send.at[j], at_recv.at[j], mate, h)
+
     def finish(j):
         def one(g, _):
             i = j * group_size + g
             full = jnp.transpose(acc[i] / sm[i])
-            attn[j, :, pl.ds(pl.multiple_of(g * DH, DH), DH)] = full.astype(jnp.bfloat16)
+            both[1, j, :, pl.ds(pl.multiple_of(g * DH, DH), DH)] = full.astype(jnp.bfloat16)
             return 0
 
         lax.fori_loop(0, group_size, one, 0)
-        copy(attn.at[j], peer.at[j], at_send.at[j], at_recv.at[j], mate, h).start()
+        attn_copy(j).start()
 
     def step(i, _):
         k = jnp.maximum(i - 2, 0)
@@ -139,16 +144,19 @@
                 for c in kv_copies(4, 3, j, kvy_send.at[2], mate):
                     c.start()
 
-        @pl.when(i == 4)
+        @pl.when((i == 4) & has_up)
         def _():
             for a in range(2):
                 right_copy(0, a).start()
 
         for at, a in ((5, 0), (8, 1)):
-            @pl.when(i == at)
+            @pl.when((i == at) & has_up)
             def _():
                 left_copy(0, a).wait_recv()
-                left_copy(1, a).start()
+
+                @pl.when(has_down)
+                def _():
+                    left_copy(1, a).start()
 
         @pl.when(s >= slot)
         def _():
@@ -195,101 +203,123 @@
 
     lax.fori_loop(0, 10, step, 0)
 
-    for t in range(1, max(n_left, n_right)):
-        for a in range(2):
-            if t < n_right:
-                right_copy(t - 1, a).wait_recv()
-                right_copy(t, a).start()
-            if 2 <= t < n_left:
-                left_copy(t - 1, a).wait_recv()
-                left_copy(t, a).start()
-    for a in range(2):
-        right_copy(n_right - 1, a).wait_recv()
-        left_copy(n_left - 1, a).wait_recv()
-
-    def attn_copy(j):
-        return copy(attn.at[j], peer.at[j], at_send.at[j], at_recv.at[j], mate, h)
-
     for j in range(2):
         attn_copy(j).wait_recv()
 
-    def first_copy(r):
-        return copy(give1.at[r], got1.at[r], s1_send.at[r], s1_recv.at[r], s, near)
-
-    def second_copy(r):
-        return copy(give2.at[r], got2.at[r], s2_send.at[r], s2_recv.at[r], s, far)
-
-    def third_copy(r):
-        return copy(give3.at[r], got3.at[r], s3_send.at[r], s3_recv.at[r], mate, h)
-
     per_side = CHUNKS // 2
 
-    def product(source, at, group, store):
-        x0 = source[0, pl.ds(at, part), :]
-        x1 = source[1, pl.ds(at, part), :]
-        for g in range(groups):
-            block = group * groups + g
-            store(g, jnp.dot(x0, wbuf[block, :half, :], preferred_element_type=jnp.float32)
-                  + jnp.dot(x1, wbuf[block, half:, :], preferred_element_type=jnp.float32))
-
-    def multiply(r, source, at):
-        for x in range(2):
-            def put(g, y, x=x):
-                give1[r, x, :, g * wc:(g + 1) * wc] = y.astype(jnp.bfloat16)
-
-            product(source, at, 2 * x + 1 - lax.rem(h, 2), put)
-        first_copy(r).start()
-        for x in range(2):
-            def hold(g, y, x=x):
-                keep[r, x, :, g * wc:(g + 1) * wc] = y
-
-            product(source, at, 2 * x + lax.rem(h, 2), hold)
-
-    mine, other = h // 2, 1 - h // 2
-
-    def second(r):
-        first_copy(r).wait_recv()
-        give2[r] = (keep[r, other] + got1[r, other].astype(jnp.float32)).astype(jnp.bfloat16)
-        second_copy(r).start()
-
-    def result(r):
-        second_copy(r).wait_recv()
-        full = keep[r, mine] + got1[r, mine].astype(jnp.float32) + got2[r].astype(jnp.float32)
-        return full.astype(jnp.bfloat16)
-
-    def place(at, member, value):
+    def first_copy(b, r):
+        return copy(sum1.at[b, r], sum1.at[b, r], s1_send.at[b, r], s1_recv.at[b, r], s, near)
+
+    def second_copy(b, r):
+        return copy(sum2.at[b, r], sum2.at[b, r], s2_send.at[b, r], s2_recv.at[b, r], s, far)
+
+    def third_copy(g, r):
+        return copy(give3.at[g, r], got3.at[g, r], s3_send.at[g, r], s3_recv.at[g, r], mate, h)
+
+    def odd(b):
+        return lax.rem(b // groups + h, 2) == 1
+
+    def block_step(e, _):
+        d = (e + 1) // 2
+        from_up = lax.rem(e, 2) == 1
+        b = jnp.where(from_up, p + d, p - d)
+        exists = (b >= 0) & (b < pairs)
+        b = jnp.clip(b, 0, pairs - 1)
+
+        @pl.when(exists & (e >= 2))
+        def _():
+            for a in range(2):
+                @pl.when(from_up)
+                def _():
+                    left_copy(d - 1, a).wait_recv()
+
+                    @pl.when(has_down)
+                    def _():
+                        left_copy(d, a).start()
+
+                @pl.when(jnp.logical_not(from_up))
+                def _():
+                    right_copy(d - 1, a).wait_recv()
+
+                    @pl.when(has_up)
+                    def _():
+                        right_copy(d, a).start()
+
+        @pl.when(exists)
+        def _():
+            away = odd(b)
+
+            def chunk(r, _):
+                side = r // per_side
+                at = pl.multiple_of(lax.rem(r, per_side) * part, part)
+                y = (jnp.dot(both[side, 0, pl.ds(at, part), :], wbuf[b, :half, :],
+                             preferred_element_type=jnp.float32)
+                     + jnp.dot(both[side, 1, pl.ds(at, part), :], wbuf[b, half:, :],
+                               preferred_element_type=jnp.float32))
+
+                @pl.when(away)
+                def _():
+                    sum1[b, r] = y.astype(jnp.bfloat16)
+                    first_copy(b, r).start()
+
+                @pl.when(jnp.logical_not(away))
+                def _():
+                    tmp[r] = y
+
+                return 0
+
+            lax.fori_loop(0, CHUNKS, chunk, 0)
+
+            @pl.when(jnp.logical_not(away))
+            def _():
+                home = b // groups == h
+                g = lax.rem(b, groups)
+
+                def settle(r, _):
+                    first_copy(b, r).wait_recv()
+                    y = tmp[r] + sum1[b, r].astype(jnp.float32)
+
+                    @pl.when(home)
+                    def _():
+                        keep[g, r] = y
+
+                    @pl.when(jnp.logical_not(home))
+                    def _():
+                        sum2[b, r] = y.astype(jnp.bfloat16)
+                        second_copy(b, r).start()
+
+                    return 0
+
+                lax.fori_loop(0, CHUNKS, settle, 0)
+
+        return 0
+
+    lax.fori_loop(0, 2 * pairs - 1, block_step, 0)
+
+    def result(g, r):
+        b = h * groups + g
+        second_copy(b, r).wait_recv()
+        return (keep[g, r] + sum2[b, r].astype(jnp.float32)).astype(jnp.bfloat16)
+
+    def place(g, at, member, value):
         for mm in range(2):
             @pl.when(member == mm)
             def _():
-                for g in range(groups):
-                    c = (2 * g + mm) * wc
-                    out_ref[pl.ds(at, part), c:c + wc] = value[:, g * wc:(g + 1) * wc]
-
-    def round_trip(r, _):
-        @pl.when(r < per_side)
-        def _():
-            multiply(r, peer, pl.multiple_of(r * part, part))
-
-        @pl.when((r >= per_side) & (r < CHUNKS))
-        def _():
-            multiply(r, attn, pl.multiple_of((r - per_side) * part, part))
-
-        @pl.when(r >= 1)
-        def _():
-            second(r - 1)
-
-        return 0
-
-    lax.fori_loop(0, CHUNKS + 1, round_trip, 0)
-
-    for r in range(per_side):
-        give3[r] = result(r)
-        third_copy(r).start()
-    for r in range(per_side, CHUNKS):
-        place((r - per_side) * part, m, result(r))
-    for r in range(per_side):
-        third_copy(r).wait_recv()
-        place(r * part, 1 - m, got3[r])
+                c = (2 * g + mm) * wc
+                out_ref[at:at + part, c:c + wc] = value
+
+    for g in range(groups):
+        for r in range(per_side):
+            give3[g, r] = result(g, r)
+            third_copy(g, r).start()
+    for g in range(groups):
+        for r in range(per_side, CHUNKS):
+            place(g, (r - per_side) * part, m, result(g, r))
+    for g in range(groups):
+        for r in range(per_side):
+            third_copy(g, r).wait_recv()
+            place(g, r * part, 1 - m, got3[g, r])
 
     for j in range(2):
         @pl.when(has_next)
@@ -318,15 +348,31 @@
                 c.wait_send()
 
         attn_copy(j).wait_send()
-        for t in range(n_left):
-            left_copy(t, j).wait_send()
-        for t in range(n_right):
-            right_copy(t, j).wait_send()
-    for r in range(CHUNKS):
-        first_copy(r).wait_send()
-        second_copy(r).wait_send()
-    for r in range(per_side):
-        third_copy(r).wait_send()
+        for t in range(pairs - 1):
+            @pl.when(has_down & (p + t < pairs))
+            def _():
+                left_copy(t, j).wait_send()
+
+            @pl.when(has_up & (p - t >= 0))
+            def _():
+                right_copy(t, j).wait_send()
+
+    def drain(b, _):
+        for r in range(CHUNKS):
+            @pl.when(odd(b))
+            def _():
+                first_copy(b, r).wait_send()
+
+            @pl.when(jnp.logical_not(odd(b)) & (b // groups != h))
+            def _():
+                second_copy(b, r).wait_send()
+
+        return 0
+
+    lax.fori_loop(0, pairs, drain, 0)
+    for g in range(groups):
+        for r in range(per_side):
+            third_copy(g, r).wait_send()
 
 
 def body(n_seq, queries, keys, values, doc_lengths, out_weight):
@@ -334,11 +380,9 @@
     kv_width = keys.shape[1]
     depth, wc = out_weight.shape
     pairs = n_seq // 2
-    n_left = pairs // 2
-    n_right = pairs - 1 - n_left
+    groups = pairs // 4
     heads = width // DH
     part = rows * 2 // CHUNKS
-    cw = pairs // 4 * wc
     slots = -(-(MOST - 1) // rows) + 1
     vmem = pl.BlockSpec(memory_space=pltpu.VMEM)
     hbm = pl.BlockSpec(memory_space=pl.ANY)
@@ -357,19 +401,18 @@
             pltpu.VMEM((heads, 1, rows), f32),
             pltpu.VMEM((heads, 1, rows), f32),
             pltpu.VMEM((heads, DH, rows), f32),
-            pltpu.VMEM((2, rows, width // 2), bf),
-            pltpu.VMEM((2, rows, width // 2), bf),
-            pltpu.VMEM((CHUNKS, 2, part, cw), bf),
-            pltpu.VMEM((CHUNKS, 2, part, cw), bf),
-            pltpu.VMEM((CHUNKS, 2, part, cw), f32),
-            pltpu.VMEM((CHUNKS, part, cw), bf),
-            pltpu.VMEM((CHUNKS, part, cw), bf),
-            pltpu.VMEM((CHUNKS // 2, part, cw), bf),
-            pltpu.VMEM((CHUNKS // 2, part, cw), bf),
+            pltpu.VMEM((2, 2, rows, width // 2), bf),
+            pltpu.VMEM((CHUNKS, part, wc), f32),
+            pltpu.VMEM((groups, CHUNKS, part, wc), f32),
+            pltpu.VMEM((pairs, CHUNKS, part, wc), bf),
+            pltpu.VMEM((pairs, CHUNKS, part, wc), bf),
+            pltpu.VMEM((groups, CHUNKS // 2, part, wc), bf),
+            pltpu.VMEM((groups, CHUNKS // 2, part, wc), bf),
             dma((3,)), dma((2, 2, 2)), dma((3, 2, 2)), dma((slots, 2, 2)),
-            dma((n_left, 2)), dma((n_left, 2)), dma((n_right, 2)), dma((n_right, 2)),
-            dma((2,)), dma((2,)), dma((CHUNKS,)), dma((CHUNKS,)),
-            dma((CHUNKS,)), dma((CHUNKS,)), dma((CHUNKS // 2,)), dma((CHUNKS // 2,)),
+            dma((pairs, 2)), dma((pairs, 2)), dma((pairs, 2)), dma((pairs, 2)),
+            dma((2,)), dma((2,)), dma((pairs, CHUNKS)), dma((pairs, CHUNKS)),
+            dma((pairs, CHUNKS)), dma((pairs, CHUNKS)),
+            dma((groups, CHUNKS // 2)), dma((groups, CHUNKS // 2)),
         ],
         compiler_params=pltpu.CompilerParams(
             collective_id=0, has_side_effects=True, vmem_limit_bytes=56 * 1024 * 1024

time: 125 us -> 133 us (1.064)
  Pallas kernels: 123 us -> 130 us
    pallas_call x1, Pallas kernels: 123 us -> 130 us  [body(): pl.pallas_call(functools.partial(kernel, n_seq), out_shape=jax.ShapeDtype...]
where the time goes in v2:
time: 133 us
  Pallas kernels  130 us (98%)
  local copies, waits for them, and re-layouts  2.26 us (2%)
    pallas_call x1, Pallas kernels, body(): pl.pallas_call(functools.partial(kernel, n_seq), out_shape=jax.ShapeDtype...  130 us

profile of v2, /device:TPU:24, one launch (start us, length us, event | category | flops | bytes accessed | tf_op | source)
XLA Modules:
  0.0 132.5 jit_solution(8631347260288467945)
XLA Ops:
  0.0 130.3 %shard_map.55 = bf16[512,1024]{1,0:T(8,128)(2,1)} custom-call(s32[16]{0:T(128)} %lens_ref.1, bf16[512,1024]{1,0:T(8,128)(2,1)} %q_ref.1, bf16[512,256]{1,0:T(8,128)(2,1)} %k_hbm.1, bf16[512,256]{1,0:T(8,128)(2,1)} %v_hbm.1, bf16[1024,512]{1,0:T(8,128)(2,1)} %w_hbm.1), custom_call_target="tpu_custom_call" | custom-call | tf_op jit(solution)/shard_map/pallas_call | solution.py:390
  130.3 2.3 %copy.7 = bf16[512,1024]{1,0:T(8,128)(2,1)} copy(bf16[512,1024]{1,0:T(8,128)(2,1)} %shard_map.55) | data formatting | bytes 2097152
